TPU v7x, 32 devices: a whole 2x2x4 slice. The times are simulated.
32 devices in a mesh: dp: 8 (over z, y), mp: 4 (over x, core).
Axes of the slice: x: 2, y: 2, z: 4, core: 2. Of those that a mesh axis runs over, the one named last changes fastest.
Arguments:
- tokens: bfloat16 [8, 1024, 1280], P('dp', 'mp'), may hold values from -6 to 6
- sizes: float32 [8, 1024], P('dp'), may hold values from 1 to 8
- ln1_gain: float32 [1280], replicated, may hold values from 0.25 to 1.75
- qkv_weight: bfloat16 [3, 1280, 1280], P(None, 'dp', 'mp'), may hold values from -0.15625 to 0.15625
- proj_weight: bfloat16 [1280, 1280], P('mp', 'dp'), may hold values from -0.15625 to 0.15625
- ln2_gain: float32 [1280], replicated, may hold values from 0.25 to 1.75
- fc1_weight: bfloat16 [1280, 5120], P('dp', 'mp'), may hold values from -0.15625 to 0.15625
- fc1_bias: float32 [5120], P('mp'), may hold values from -3 to 3
- fc2_weight: bfloat16 [5120, 1280], P('mp', 'dp'), may hold values from -0.078125 to 0.078125
- pair_source: int32 [8, 16], P('dp'), may hold values from 0 to 1022, as said below
- pair_target: int32 [8, 16], P('dp'), may hold values from 1 to 1023, as said below
- kept_order: int32 [8, 1008], P('dp'), may hold values from 0 to 1023, as said below
Outputs:
- merged_out: bfloat16 [8, 1008, 1280], P('dp', 'mp')
Inputs may be any that keep to these rules, and one draw needn't show every extreme that they name: `pair_source`: in each image the 16 entries are distinct even token indices. `pair_target`: odd token indices; several sources may join the same target. `kept_order`: in each image every token index that is not in pair_source appears exactly once.
All inputs are finite; a program needn't handle non-finite values.
Results may differ from a plain program's by a relative error of at most 0.017.
Values may be sent and summed in bfloat16 or wider, within the bound.
A program may use at most 64 MiB of HBM per device.

v0:
```python
import math
import jax
import jax.numpy as jnp
from jax import lax
from jax.sharding import PartitionSpec as P

D = 1280
HEADS = 16


def layer_norm(values, gain):
    center = values - jnp.mean(values, axis=-1, keepdims=True)
    spread = jnp.mean(center * center, axis=-1, keepdims=True)
    return center * lax.rsqrt(spread + 1e-06) * gain


def merge_rows(total, order_rows, source_ids, target_ids):
    kept_rows = jnp.take_along_axis(total, order_rows[:, :, None], axis=1)
    source_rows = jnp.take_along_axis(total, source_ids[:, :, None], axis=1)
    joins = (order_rows[:, :, None] == target_ids[:, None, :]).astype(jnp.float32)
    return kept_rows + jnp.einsum(
        "icr,ird->icd", joins, source_rows, precision=lax.Precision.HIGHEST
    )


def shards(
    tokens,
    sizes,
    ln1_gain,
    qkv_weight,
    proj_weight,
    ln2_gain,
    fc1_weight,
    fc1_bias,
    fc2_weight,
    pair_source,
    pair_target,
    kept_order,
):
    images, own_tokens, width = tokens.shape
    length = sizes.shape[1]
    kept_total = kept_order.shape[1]
    devices_mp = lax.axis_size("mp")
    own_start = lax.axis_index("mp") * own_tokens
    head_size = D // HEADS
    base = tokens.astype(jnp.float32)
    normed = layer_norm(base, ln1_gain).astype(jnp.bfloat16)
    whole = lax.all_gather(normed, "mp", axis=1, tiled=True)
    local_width = qkv_weight.shape[2]
    columns = whole
    projected = jnp.einsum(
        "ind,cdf->cinf",
        columns,
        lax.all_gather(qkv_weight, "dp", axis=1, tiled=True),
        preferred_element_type=jnp.float32,
    ).astype(jnp.bfloat16)
    local_heads = local_width // head_size
    shaped = projected.reshape(3, images, length, local_heads, head_size)
    queries = shaped[0]
    keys_all = shaped[1]
    values_all = shaped[2]
    size_bias = jnp.log(sizes)[:, None, None, :]
    block = min(512, length)
    outputs = []
    for begin in range(0, length, block):
        scores = (
            jnp.einsum(
                "iqhe,ikhe->ihqk",
                queries[:, begin : begin + block],
                keys_all,
                preferred_element_type=jnp.float32,
            )
            / math.sqrt(head_size)
            + size_bias
        )
        weights = jax.nn.softmax(scores, axis=-1).astype(jnp.bfloat16)
        attended_block = jnp.einsum(
            "ihqk,ikhe->iqhe", weights, values_all, preferred_element_type=jnp.float32
        )
        outputs.append(attended_block.astype(jnp.bfloat16).reshape(images, block, local_width))
    attended = jnp.concatenate(outputs, axis=1)
    branch = jnp.einsum(
        "ind,de->ine",
        attended,
        lax.all_gather(proj_weight, "dp", axis=1, tiled=True),
        preferred_element_type=jnp.float32,
    )
    weighted = sizes[:, :, None] * branch
    own_sizes = lax.dynamic_slice_in_dim(sizes, own_start, own_tokens, 1)
    own_weighted = own_sizes[:, :, None] * base
    local_total = lax.dynamic_update_slice_in_dim(
        weighted,
        lax.dynamic_slice_in_dim(weighted, own_start, own_tokens, 1) + own_weighted,
        own_start,
        1,
    )
    merged_count = kept_total // devices_mp
    own_order = lax.dynamic_slice_in_dim(
        kept_order, lax.axis_index("mp") * merged_count, merged_count, 1
    )
    scattered = lax.psum_scatter(
        jnp.transpose(
            merge_rows(local_total, kept_order, pair_source, pair_target), (1, 0, 2)
        ).astype(jnp.bfloat16),
        "mp",
        scatter_dimension=0,
        tiled=True,
    ).astype(jnp.float32)
    numerator = jnp.transpose(scattered, (1, 0, 2))
    merged_size = merge_rows(sizes[:, :, None], own_order, pair_source, pair_target)
    merged = numerator / merged_size
    normed_two = layer_norm(merged, ln2_gain).astype(jnp.bfloat16)
    gathered = lax.all_gather(normed_two, "mp", axis=1, tiled=True)
    columns = gathered
    hidden_sum = jnp.einsum(
        "imd,df->imf",
        columns,
        lax.all_gather(fc1_weight, "dp", axis=0, tiled=True),
        preferred_element_type=jnp.float32,
    )
    hidden = jax.nn.gelu(hidden_sum + fc1_bias).astype(jnp.bfloat16)
    partial_out = jnp.einsum(
        "imf,fd->imd",
        hidden,
        lax.all_gather(fc2_weight, "dp", axis=1, tiled=True),
        preferred_element_type=jnp.float32,
    )
    mlp_part = lax.psum_scatter(
        partial_out.astype(jnp.bfloat16), "mp", scatter_dimension=1, tiled=True
    ).astype(jnp.float32)
    return (merged + mlp_part).astype(jnp.bfloat16)


def solution(mesh):
    return jax.shard_map(
        shards,
        mesh=mesh,
        in_specs=(
            P("dp", "mp", None),
            P("dp", None),
            P(),
            P(None, "dp", "mp"),
            P("mp", "dp"),
            P(),
            P("dp", "mp"),
            P("mp"),
            P("mp", "dp"),
            P("dp", None),
            P("dp", None),
            P("dp", None),
        ),
        out_specs=P("dp", "mp", None),
        check_vma=False,
    )
```

profile of v0, /device:TPU:1, one launch (start us, length us, event | category | flops | bytes accessed | tf_op | source)
XLA Modules:
  0.0 317.7 jit_solution(4380768634615341311)
XLA Ops:
  6.5 0.0 all-gather.6.cloned.1.call-start
  6.6 1.3 convert_reduce_fusion
  7.9 0.0 copy-start.5
  7.9 1.4 fusion.30
  9.3 2.2 fusion.32
  11.5 0.0 all-gather.6.cloned.1.call-update
  11.6 0.0 all-gather.8.cloned.1.call-start
  11.6 0.7 all-gather.8.cloned.1.call-update
  12.3 0.0 all-gather.12.cloned.1.call-start
  12.4 0.7 all-gather.12.cloned.1.call-update
  13.0 0.0 all-gather.14.cloned.1.call-start
  13.1 0.5 all-gather.14.cloned.1.call-update
  13.6 0.0 all-gather.10.cloned.1.call-start
  13.7 0.0 copy-done.8
  13.7 0.0 copy-done
  13.7 0.0 copy-done.2
  13.8 28.3 %all_gather.20 = bf16[320,1280]{0,1:T(8,128)(2,1)S(1)} all-gather(bf16[320,160]{0,1:T(8,128)(2,1)S(1)} %copy-done.2), channel_id=1, replica_groups=mesh['dp'=8,'mp'=4] {'dp'}, dimensions={1}, use_global_device_ids=true | all-gather | bytes 921600 | tf_op jit(solution)/shard_map/all_gather | solution.py:85
  42.0 0.0 copy-done.3
  42.1 0.1 compare_select_fusion.2
  42.2 0.6 gather_fusion.3
  42.8 1.4 gather_fusion.2
  44.2 0.0 copy-done.5
  44.2 0.2 fusion.56
  44.4 53.4 %all-gather.8.cloned.1.call-done = bf16[3,1280,320]{2,1,0:T(8,128)(2,1)} async-done(((bf16[3,160,320]{2,1,0:T(8,128)(2,1)}), bf16[3,1280,320]{2,1,0:T(8,128)(2,1)}) %all-gather.8.cloned.1.call-update) | async-done | bytes 2457616 | tf_op jit(solution)/shard_map/all_gather | solution.py:54
  97.8 5.4 %convert_bitcast_fusion = bf16[3,1,1024,320]{2,3,0,1:T(8,128)(2,1)S(1)} fusion(bf16[3,1280,320]{2,1,0:T(8,128)(2,1)} %all-gather.8.cloned.1.call-done, bf16[1,1024,1280]{2,1,0:T(8,128)(2,1)} %all-gather.6.cloned.1.call-done), kind=kOutput, calls=%fused_computation.38 | convolution fusion | flops 2517565440 | bytes 7045120 | tf_op jit(solution)/shard_map/ind,cdf->cinf/dot_general | solution.py:51
  103.2 0.2 fusion.78
  103.3 4.9 %fusion.80 = (f32[4,512]{1,0:T(4,128)S(1)}, f32[4,512,1024]{2,1,0:T(8,128)}) fusion(f32[1024]{0:T(1024)S(1)} %bitcast.179, bf16[1024,4,80]{0,2,1:T(8,128)(2,1)S(1)} %bitcast.170, bf16[1,1024,4,80]{1,3,2,0:T(8,128)(2,1)S(1)} %bitcast.168), kind=kOutput, calls=%fused_computation.120 | convolution fusion | flops 343933952 | bytes 9383936 | tf_op jit(solution)/shard_map/sub | solution.py:76
  108.2 4.9 %fusion.79 = (f32[4,512]{1,0:T(4,128)S(1)}, f32[4,512,1024]{2,1,0:T(8,128)}) fusion(f32[1024]{0:T(1024)S(1)} %bitcast.180, bf16[1024,4,80]{0,2,1:T(8,128)(2,1)S(1)} %bitcast.171, bf16[1,1024,4,80]{1,3,2,0:T(8,128)(2,1)S(1)} %bitcast.169), kind=kOutput, calls=%fused_computation.119 | convolution fusion | flops 343933952 | bytes 9383936 | tf_op jit(solution)/shard_map/sub | solution.py:76
  113.0 5.1 %fusion.37 = bf16[4,80,512]{2,1,0:T(8,128)(2,1)S(1)} fusion(bf16[1024,4,80]{0,2,1:T(8,128)(2,1)S(1)} %bitcast.166, f32[4,512,1024]{2,1,0:T(8,128)} %get-tuple-element.13, f32[4,512]{1,0:T(4,128)S(1)} %get-tuple-element.12), kind=kOutput, calls=%fused_computation.55 | convolution fusion | flops 339902464 | bytes 9379840 | tf_op jit(solution)/shard_map/ihqk,ikhe->iqhe/dot_general | solution.py:77
  118.1 0.8 copy-done.9
  118.9 1.7 fusion.36
  120.6 0.0 copy-start.1
  120.6 4.0 %convolution_multiply_fusion = f32[1024,1280]{1,0:T(8,128)} fusion(bf16[320,1280]{0,1:T(8,128)(2,1)S(1)} %all_gather.20, f32[1024]{0:T(1024)S(1)} %bitcast.165, bf16[1,512,320]{1,2,0:T(8,128)(2,1)S(1)} %bitcast.173, bf16[1,512,320]{1,2,0:T(8,128)(2,1)S(1)} %bitcast.172), kind=kOutput, calls=%fused_computation.24 | convolution fusion | flops 841482240 | bytes 6721536 | tf_op jit(solution)/shard_map/ind,de->ine/dot_general | solution.py:82
  124.6 1.4 constant_dynamic-slice_fusion.2
  126.0 0.0 copy-done.1
  126.0 1.3 fusion.35
  127.3 3.1 gather_fusion.1
  130.5 9.7 %gather_fusion = f32[1008,1280]{1,0:T(8,128)} fusion(f32[1024,1280]{1,0:T(8,128)} %fusion.35, s32[1024]{0:T(1024)S(1)} %pad_clamp_fusion.2), kind=kCustom, calls=%fused_computation | custom fusion | bytes 10325952 | tf_op jit(solution)/shard_map/jit(take_along_axis)/gather | solution.py:18
  140.1 5.1 %fusion.21 = bf16[1008,1,1280]{2,0,1:T(8,128)(2,1)S(1)} fusion(f32[1008,1280]{1,0:T(8,128)} %gather_fusion, pred[1008]{0:T(1024)(128)(4,1)S(1)} %compare_and_fusion, f32[16,1280]{1,0:T(8,128)S(1)} %gather_fusion.1, pred[16]{0:T(512)(128)(4,1)S(1)} %compare_and_fusion.1, s32[1008]{0:T(1024)S(1)} %bitcast.175, s32[16]{0:T(128)S(1)} %bitcast.185), kind=kOutput, calls=%fused_computation.33 | convolution fusion | flops 251633408 | bytes 7828480 | tf_op jit(solution)/shard_map/icr,ird->icd/dot_general | solution.py:21
  145.2 0.0 copy-start.6
  145.2 0.0 copy-start.4
  145.2 27.6 %fusion = bf16[256,1280]{1,0:T(8,128)(2,1)S(1)} fusion(bf16[1008,1,1280]{2,0,1:T(8,128)(2,1)S(1)} %fusion.21), kind=kCustom, calls=%all-reduce-scatter | all-reduce-scatter fusion | flops 1310721 | bytes 3236352
  172.8 4.4 %collective-permute-start = (bf16[12,1280]{1,0:T(8,128)(2,1)S(1)}, bf16[12,1280]{1,0:T(8,128)(2,1)S(1)}, u32[]{:S(2)}, u32[]{:S(2)}) collective-permute-start(bf16[12,1280]{1,0:T(8,128)(2,1)S(1)} %slice.36), channel_id=1, source_target_pairs={{0,1},{1,2},{2,3},{4,5},{5,6},{6,7},{8,9},{9,10},{10,11},{12,13},{... | collective-permute-start | bytes 92168
  177.2 0.0 copy-done.6
  177.2 0.6 dynamic-slice.10
  178.5 0.0 collective-permute-done
  178.5 1.1 concatenate.4
  179.6 0.0 copy-start.7
  179.6 0.4 fusion.46
  180.0 0.5 multiply_reduce_fusion
  180.5 0.0 copy-done.4
  180.5 0.4 multiply_convert_fusion
  180.9 2.1 copy.14
  183.0 0.0 all-gather.10.cloned.1.call-update
  183.0 0.0 all-gather.12.cloned.1.call-done
  183.1 39.2 %all-gather.14.cloned.1.call-done = bf16[1280,1280]{0,1:T(8,128)(2,1)} async-done(((bf16[1280,160]{0,1:T(8,128)(2,1)}), bf16[1280,1280]{0,1:T(8,128)(2,1)}) %all-gather.14.cloned.1.call-update) | async-done | bytes 3276816 | tf_op jit(solution)/shard_map/all_gather | solution.py:125
  222.2 42.2 %all-gather.10.cloned.1.call-done = bf16[1,1008,1280]{2,0,1:T(2,128)(2,1)} async-done(((bf16[1,252,1280]{2,0,1:T(2,128)(2,1)}), bf16[1,1008,1280]{2,0,1:T(2,128)(2,1)}) %all-gather.10.cloned.1.call-update) | async-done | bytes 2580496 | tf_op jit(solution)/shard_map/all_gather | solution.py:113
  264.5 0.0 copy-done.7
  264.5 12.8 %fusion.20 = bf16[1,1008,1280]{2,1,0:T(8,128)(2,1)} fusion(bf16[1280,1280]{0,1:T(8,128)(2,1)} %all-gather.14.cloned.1.call-done, bf16[1280,1280]{1,0:T(8,128)(2,1)} %all-gather.12.cloned.1.call-done, bf16[1,1008,1280]{2,0,1:T(2,128)(2,1)} %all-gather.10.cloned.1.call-done, f32[1280]{0:T(1024)S(1)} %copy-done.7), kind=kOutput, calls=%fused_computation.32 | convolution fusion | flops 6620221440 | bytes 11719680 | tf_op jit(solution)/shard_map/imf,fd->imd/dot_general | solution.py:122
  277.3 26.0 %fusion.1 = bf16[256,1280]{1,0:T(8,128)(2,1)S(1)} fusion(bf16[1,1008,1280]{2,1,0:T(8,128)(2,1)} %fusion.20), kind=kCustom, calls=%all-reduce-scatter.1 | all-reduce-scatter fusion | flops 1310721 | bytes 3236352
  303.4 4.4 %collective-permute-start.1 = (bf16[12,1280]{1,0:T(8,128)(2,1)S(1)}, bf16[12,1280]{1,0:T(8,128)(2,1)S(1)}, u32[]{:S(2)}, u32[]{:S(2)}) collective-permute-start(bf16[12,1280]{1,0:T(8,128)(2,1)S(1)} %slice.37), channel_id=1, source_target_pairs={{0,1},{1,2},{2,3},{4,5},{5,6},{6,7},{8,9},{9,10},{10,11},{12,13},{... | collective-permute-start | bytes 92168
  307.8 1.1 collective-permute-done.1
  308.9 1.0 concatenate.5
  309.9 1.3 add_convert_fusion.1
  (22 shorter events, 0.1 us)
Async XLA Ops:
  6.5 7.1 %copy-start.8 = (s32[1,16]{1,0:T(1,128)S(1)}, s32[1,16]{1,0:T(1,128)}, u32[]{:S(2)}) copy-start(s32[1,16]{1,0:T(1,128)} %param.21) | copy-start | bytes 196
  6.5 7.2 %copy-start = (f32[1,1024]{1,0:T(1,128)S(1)}, f32[1,1024]{1,0:T(1,128)}, u32[]{:S(2)}) copy-start(f32[1,1024]{1,0:T(1,128)} %param.13) | copy-start | bytes 12292
  6.5 7.2 %copy-start.2 = (bf16[320,160]{0,1:T(8,128)(2,1)S(1)}, bf16[320,160]{0,1:T(8,128)(2,1)}, u32[]{:S(2)}) copy-start(bf16[320,160]{0,1:T(8,128)(2,1)} %param.16) | copy-start | bytes 307204
  6.5 35.5 %copy-start.3 = (s32[1,1008]{1,0:T(1,128)S(1)}, s32[1,1008]{1,0:T(1,128)}, u32[]{:S(2)}) copy-start(s32[1,1008]{1,0:T(1,128)} %param.23) | copy-start | bytes 12100
  6.5 37.8 %all-gather.6.cloned.1.call-start = ((), (), s32[]{:S(2)}) async-start(), calls=%async_computation | async-start | bytes 3276800 | tf_op jit(solution)/shard_map/all_gather | solution.py:48
  7.9 36.3 %copy-start.5 = (s32[1,16]{1,0:T(1,128)S(1)}, s32[1,16]{1,0:T(1,128)}, u32[]{:S(2)}) copy-start(s32[1,16]{1,0:T(1,128)} %param.22) | copy-start | bytes 196
  11.6 86.2 %all-gather.8.cloned.1.call-start = ((), (), s32[]{:S(2)}) async-start(), calls=%async_computation.1 | async-start | bytes 3317760 | tf_op jit(solution)/shard_map/all_gather | solution.py:54
  12.3 170.7 %all-gather.12.cloned.1.call-start = ((), (), s32[]{:S(2)}) async-start(), calls=%async_computation.3 | async-start | bytes 3686400 | tf_op jit(solution)/shard_map/all_gather | solution.py:118
  13.0 209.2 %all-gather.14.cloned.1.call-start = ((), (), s32[]{:S(2)}) async-start(), calls=%async_computation.4 | async-start | bytes 3686400 | tf_op jit(solution)/shard_map/all_gather | solution.py:125
  13.6 250.8 %all-gather.10.cloned.1.call-start = ((), (), s32[]{:S(2)}) async-start(), calls=%async_computation.2 | async-start | bytes 6451200 | tf_op jit(solution)/shard_map/all_gather | solution.py:113
  113.0 5.9 %copy-start.9 = (f32[4,512,1024]{2,1,0:T(8,128)S(1)}, f32[4,512,1024]{2,1,0:T(8,128)}, u32[]{:S(2)}) copy-start(f32[4,512,1024]{2,1,0:T(8,128)} %get-tuple-element.11) | copy-start | bytes 25165828
  120.6 5.4 %copy-start.1 = (bf16[1,256,1280]{2,1,0:T(8,128)(2,1)S(1)}, bf16[1,256,1280]{2,1,0:T(8,128)(2,1)}, u32[]{:S(2)}) copy-start(bf16[1,256,1280]{2,1,0:T(8,128)(2,1)} %param.12) | copy-start | bytes 1966084
  145.2 32.0 %copy-start.6 = (u32[32]{0:T(128)S(1)}, u32[32]{0:T(128)}, u32[]{:S(2)}) copy-start(u32[32]{0:T(128)} %constant.99) | copy-start | bytes 388
  145.2 35.3 %copy-start.4 = (f32[1280]{0:T(1024)S(1)}, f32[1280]{0:T(1024)}, u32[]{:S(2)}) copy-start(f32[1280]{0:T(1024)} %param.17) | copy-start | bytes 15364
  172.8 5.7 %collective-permute-start = (bf16[12,1280]{1,0:T(8,128)(2,1)S(1)}, bf16[12,1280]{1,0:T(8,128)(2,1)S(1)}, u32[]{:S(2)}, u32[]{:S(2)}) collective-permute-start(bf16[12,1280]{1,0:T(8,128)(2,1)S(1)} %slice.36), channel_id=1, source_target_pairs={{0,1},{1,2},{2,3},{4,5},{5,6},{6,7},{8,9},{9,10},{10,11},{12,13},{... | collective-permute-start | bytes 92168
  179.6 84.9 %copy-start.7 = (f32[1280]{0:T(1024)S(1)}, f32[1280]{0:T(1024)}, u32[]{:S(2)}) copy-start(f32[1280]{0:T(1024)} %param.19) | copy-start | bytes 15364
  303.4 5.5 %collective-permute-start.1 = (bf16[12,1280]{1,0:T(8,128)(2,1)S(1)}, bf16[12,1280]{1,0:T(8,128)(2,1)S(1)}, u32[]{:S(2)}, u32[]{:S(2)}) collective-permute-start(bf16[12,1280]{1,0:T(8,128)(2,1)S(1)} %slice.37), channel_id=1, source_target_pairs={{0,1},{1,2},{2,3},{4,5},{5,6},{6,7},{8,9},{9,10},{10,11},{12,13},{... | collective-permute-start | bytes 92168
Sparse Core Ops, SparseCore 0:
  11.7 27.9 all-gather.5
  41.9 55.8 all-gather.7
  100.0 59.9 all-gather.11
  162.0 60.1 all-gather.13
  223.6 40.7 all-gather.9
where the time goes:
time: 318 us
  waiting for transfers between devices  138 us (43%)
  blocking collectives  81.9 us (26%)
  matrix products  44 us (14%)
  local copies, waits for them, and re-layouts  22 us (7%)
  between operations  14.1 us (4%)
  starting transfers between devices  8.96 us (3%)
  other arithmetic  8.93 us (3%)
    unnamed x2, blocking collectives  53.6 us
    all_gather x1, waiting for transfers between devices, shards(): lax.all_gather(qkv_weight, 'dp', axis=1, tiled=True)  53.4 us
    all_gather x1, waiting for transfers between devices, shards(): gathered = lax.all_gather(normed_two, 'mp', axis=1, tiled=True)  42.2 us
    all_gather x1, waiting for transfers between devices, shards(): lax.all_gather(fc2_weight, 'dp', axis=1, tiled=True)  39.2 us
    all_gather x1, blocking collectives, shards(): lax.all_gather(proj_weight, 'dp', axis=1, tiled=True)  28.3 us
    dot_general x1, matrix products, shards(): jnp.einsum('imf,fd->imd', hidden, lax.all_gather(fc2_weight, 'dp', axis=1...  12.8 us
    gather x2, local copies, waits for them, and re-layouts, merge_rows(): kept_rows = jnp.take_along_axis(total, order_rows[:, :, None], axis=1)  11 us
    sub x2, matrix products, shards(): weights = jax.nn.softmax(scores, axis=-1).astype(jnp.bfloat16)  9.7 us
  transfers between devices with their start and end apart: 7, of which 4 were waited for; matrix products, arithmetic and copies ran while one was open for 26% of the time, Pallas kernels for 0%

commit v1 on v0

--- a/solution.py
+++ b/solution.py
@@ -110,7 +110,7 @@
     merged_size = merge_rows(sizes[:, :, None], own_order, pair_source, pair_target)
     merged = numerator / merged_size
     normed_two = layer_norm(merged, ln2_gain).astype(jnp.bfloat16)
-    gathered = lax.all_gather(normed_two, "mp", axis=1, tiled=True)
+    gathered = jnp.concatenate(lax.all_gather(normed_two, "mp"), axis=1)
     columns = gathered
     hidden_sum = jnp.einsum(
         "imd,df->imf",

time: 318 us -> 384 us (1.21)
  waiting for transfers between devices: 138 us -> 203 us
    all_gather x1, waiting for transfers between devices: 0.02 us -> 59.4 us  [shards(): lax.all_gather(fc1_weight, 'dp', axis=0, tiled=True)]
    all_gather x1, waiting for transfers between devices: 39.2 us -> 62.2 us  [shards(): lax.all_gather(fc2_weight, 'dp', axis=1, tiled=True)]
    all_gather x1, waiting for transfers between devices: 42.2 us -> 23.9 us  [shards(): gathered = jnp.concatenate(lax.all_gather(normed_two, 'mp'), axis=1)]
  transfers between devices with their start and end apart: 7 -> 7, of which waited for: 4 -> 5; matrix products, arithmetic and copies ran while one was open for 26% -> 1% of each run, Pallas kernels for 0% -> 0%
where the time goes in v1:
time: 384 us
  waiting for transfers between devices  203 us (53%)
  blocking collectives  83.5 us (22%)
  matrix products  42.9 us (11%)
  local copies, waits for them, and re-layouts  21.7 us (6%)
  between operations  14.1 us (4%)
  other arithmetic  9.75 us (3%)
  starting transfers between devices  8.97 us (2%)
    all_gather x1, waiting for transfers between devices, shards(): lax.all_gather(fc2_weight, 'dp', axis=1, tiled=True)  62.2 us
    all_gather x1, waiting for transfers between devices, shards(): lax.all_gather(fc1_weight, 'dp', axis=0, tiled=True)  59.4 us
    unnamed x2, blocking collectives  55.1 us
    all_gather x1, waiting for transfers between devices, shards(): lax.all_gather(qkv_weight, 'dp', axis=1, tiled=True)  54.6 us
    all_gather x1, blocking collectives, shards(): lax.all_gather(proj_weight, 'dp', axis=1, tiled=True)  28.3 us
    all_gather x1, waiting for transfers between devices, shards(): gathered = jnp.concatenate(lax.all_gather(normed_two, 'mp'), axis=1)  23.9 us
    dot_general x1, matrix products, shards(): jnp.einsum('imf,fd->imd', hidden, lax.all_gather(fc2_weight, 'dp', axis=1...  11.7 us
    gather x2, local copies, waits for them, and re-layouts, merge_rows(): kept_rows = jnp.take_along_axis(total, order_rows[:, :, None], axis=1)  10.9 us
  transfers between devices with their start and end apart: 7, of which 5 were waited for; matrix products, arithmetic and copies ran while one was open for 1% of the time, Pallas kernels for 0%

profile of v1, /device:TPU:1, one launch (start us, length us, event | category | flops | bytes accessed | tf_op | source)
XLA Modules:
  0.0 383.9 jit_solution(10635563699653789839)
XLA Ops:
  6.5 0.0 copy-start
  6.5 0.0 copy-start.8
  6.5 0.0 all-gather.6.cloned.1.call-start
  6.6 1.3 convert_reduce_fusion
  7.9 1.4 fusion.28
  9.3 2.2 fusion.30
  11.5 0.0 all-gather.6.cloned.1.call-update
  11.6 0.0 all-gather.8.cloned.1.call-start
  11.6 0.7 all-gather.8.cloned.1.call-update
  12.3 0.0 all-gather.10.cloned.1.call-start
  12.4 0.0 copy-done
  12.4 0.0 copy-done.8
  12.4 0.6 gather_fusion.3
  13.1 0.0 copy-done.3
  13.1 0.1 compare_select_fusion.2
  13.2 1.4 gather_fusion.2
  14.6 0.0 copy-done.5
  14.6 0.2 fusion.58
  14.8 0.0 copy-done.2
  14.8 28.3 %all_gather.21 = bf16[320,1280]{0,1:T(8,128)(2,1)S(1)} all-gather(bf16[320,160]{0,1:T(8,128)(2,1)S(1)} %copy-done.2), channel_id=1, replica_groups=mesh['dp'=8,'mp'=4] {'dp'}, dimensions={1}, use_global_device_ids=true | all-gather | bytes 921600 | tf_op jit(solution)/shard_map/all_gather | solution.py:85
  43.2 54.6 %all-gather.8.cloned.1.call-done = bf16[3,1280,320]{2,1,0:T(8,128)(2,1)} async-done(((bf16[3,160,320]{2,1,0:T(8,128)(2,1)}), bf16[3,1280,320]{2,1,0:T(8,128)(2,1)}) %all-gather.8.cloned.1.call-update) | async-done | bytes 2457616 | tf_op jit(solution)/shard_map/all_gather | solution.py:54
  97.8 5.4 %convert_bitcast_fusion = bf16[3,1,1024,320]{2,3,0,1:T(8,128)(2,1)S(1)} fusion(bf16[3,1280,320]{2,1,0:T(8,128)(2,1)} %all-gather.8.cloned.1.call-done, bf16[1,1024,1280]{2,1,0:T(8,128)(2,1)} %all-gather.6.cloned.1.call-done), kind=kOutput, calls=%fused_computation.36 | convolution fusion | flops 2517565440 | bytes 7045120 | tf_op jit(solution)/shard_map/ind,cdf->cinf/dot_general | solution.py:51
  103.2 0.2 fusion.80
  103.3 5.0 %fusion.82 = (f32[4,512]{1,0:T(4,128)S(1)}, f32[4,512,1024]{2,1,0:T(8,128)}) fusion(f32[1024]{0:T(1024)S(1)} %bitcast.181, bf16[1024,4,80]{0,2,1:T(8,128)(2,1)S(1)} %bitcast.172, bf16[1,1024,4,80]{1,3,2,0:T(8,128)(2,1)S(1)} %bitcast.170), kind=kOutput, calls=%fused_computation.123 | convolution fusion | flops 343933952 | bytes 9383936 | tf_op jit(solution)/shard_map/sub | solution.py:76
  108.4 4.9 %fusion.81 = (f32[4,512]{1,0:T(4,128)S(1)}, f32[4,512,1024]{2,1,0:T(8,128)}) fusion(f32[1024]{0:T(1024)S(1)} %bitcast.182, bf16[1024,4,80]{0,2,1:T(8,128)(2,1)S(1)} %bitcast.173, bf16[1,1024,4,80]{1,3,2,0:T(8,128)(2,1)S(1)} %bitcast.171), kind=kOutput, calls=%fused_computation.122 | convolution fusion | flops 343933952 | bytes 9383936 | tf_op jit(solution)/shard_map/sub | solution.py:76
  113.2 5.0 %fusion.41 = bf16[4,80,512]{2,1,0:T(8,128)(2,1)S(1)} fusion(bf16[1024,4,80]{0,2,1:T(8,128)(2,1)S(1)} %bitcast.168, f32[4,512,1024]{2,1,0:T(8,128)} %get-tuple-element.13, f32[4,512]{1,0:T(4,128)S(1)} %get-tuple-element.12), kind=kOutput, calls=%fused_computation.59 | convolution fusion | flops 339902464 | bytes 9379840 | tf_op jit(solution)/shard_map/ihqk,ikhe->iqhe/dot_general | solution.py:77
  118.2 0.7 copy-done.9
  119.0 1.7 fusion.40
  120.7 0.0 copy-start.1
  120.7 4.0 %convolution_multiply_fusion = f32[1024,1280]{1,0:T(8,128)} fusion(bf16[320,1280]{0,1:T(8,128)(2,1)S(1)} %all_gather.21, f32[1024]{0:T(1024)S(1)} %bitcast.167, bf16[1,512,320]{1,2,0:T(8,128)(2,1)S(1)} %bitcast.175, bf16[1,512,320]{1,2,0:T(8,128)(2,1)S(1)} %bitcast.174), kind=kOutput, calls=%fused_computation.24 | convolution fusion | flops 841482240 | bytes 6721536 | tf_op jit(solution)/shard_map/ind,de->ine/dot_general | solution.py:82
  124.7 1.4 constant_dynamic-slice_fusion.2
  126.1 0.0 copy-done.1
  126.1 1.3 fusion.39
  127.4 3.1 gather_fusion.1
  130.6 9.5 %gather_fusion = f32[1008,1280]{1,0:T(8,128)} fusion(f32[1024,1280]{1,0:T(8,128)} %fusion.39, s32[1024]{0:T(1024)S(1)} %pad_clamp_fusion.2), kind=kCustom, calls=%fused_computation | custom fusion | bytes 10325952 | tf_op jit(solution)/shard_map/jit(take_along_axis)/gather | solution.py:18
  140.1 5.1 %fusion.21 = bf16[1008,1,1280]{2,0,1:T(8,128)(2,1)S(1)} fusion(f32[1008,1280]{1,0:T(8,128)} %gather_fusion, pred[1008]{0:T(1024)(128)(4,1)S(1)} %compare_and_fusion, f32[16,1280]{1,0:T(8,128)S(1)} %gather_fusion.1, pred[16]{0:T(512)(128)(4,1)S(1)} %compare_and_fusion.1, s32[1008]{0:T(1024)S(1)} %bitcast.177, s32[16]{0:T(128)S(1)} %bitcast.187), kind=kOutput, calls=%fused_computation.33 | convolution fusion | flops 251633408 | bytes 7828480 | tf_op jit(solution)/shard_map/icr,ird->icd/dot_general | solution.py:21
  145.1 0.0 copy-start.6
  145.1 0.0 copy-start.4
  145.2 27.3 %fusion = bf16[256,1280]{1,0:T(8,128)(2,1)S(1)} fusion(bf16[1008,1,1280]{2,0,1:T(8,128)(2,1)S(1)} %fusion.21), kind=kCustom, calls=%all-reduce-scatter | all-reduce-scatter fusion | flops 1310721 | bytes 3236352
  172.5 4.4 %collective-permute-start = (bf16[12,1280]{1,0:T(8,128)(2,1)S(1)}, bf16[12,1280]{1,0:T(8,128)(2,1)S(1)}, u32[]{:S(2)}, u32[]{:S(2)}) collective-permute-start(bf16[12,1280]{1,0:T(8,128)(2,1)S(1)} %slice.36), channel_id=1, source_target_pairs={{0,1},{1,2},{2,3},{4,5},{5,6},{6,7},{8,9},{9,10},{10,11},{12,13},{... | collective-permute-start | bytes 92168
  176.9 0.0 copy-done.6
  176.9 0.6 dynamic-slice.10
  178.1 0.0 collective-permute-done
  178.2 1.1 concatenate.4
  179.2 0.4 fusion.48
  179.7 0.5 multiply_reduce_fusion
  180.1 0.0 copy-done.4
  180.1 1.2 fusion.36
  181.4 0.0 all-gather.10.cloned.1.call-update
  181.4 0.0 all-gather.12.cloned.1.call-start
  181.5 0.5 all-gather.12.cloned.1.call-update
  182.0 0.0 all-gather.14.cloned.1.call-start
  182.0 0.5 all-gather.14.cloned.1.call-update
  182.6 23.9 %all-gather.10.cloned.1.call-done = bf16[4,1,252,1280]{3,2,1,0:T(8,128)(2,1)} async-done(((bf16[1,1,252,1280]{3,2,1,0:T(8,128)(2,1)}), bf16[4,1,252,1280]{3,2,1,0:T(8,128)(2,1)}) %all-gather.10.cloned.1.call-update) | async-done | bytes 2580496 | tf_op jit(solution)/shard_map/all_gather | solution.py:113
  206.5 2.0 reshape.869
  208.5 59.4 %all-gather.12.cloned.1.call-done = bf16[1280,1280]{1,0:T(8,128)(2,1)} async-done(((bf16[160,1280]{1,0:T(8,128)(2,1)}), bf16[1280,1280]{1,0:T(8,128)(2,1)}) %all-gather.12.cloned.1.call-update) | async-done | bytes 3276816 | tf_op jit(solution)/shard_map/all_gather | solution.py:118
  267.8 62.2 %all-gather.14.cloned.1.call-done = bf16[1280,1280]{0,1:T(8,128)(2,1)} async-done(((bf16[1280,160]{0,1:T(8,128)(2,1)}), bf16[1280,1280]{0,1:T(8,128)(2,1)}) %all-gather.14.cloned.1.call-update) | async-done | bytes 3276816 | tf_op jit(solution)/shard_map/all_gather | solution.py:125
  330.0 0.0 copy-done.7
  330.0 11.7 %fusion.20 = bf16[1,1008,1280]{2,1,0:T(8,128)(2,1)} fusion(bf16[1280,1280]{0,1:T(8,128)(2,1)} %all-gather.14.cloned.1.call-done, bf16[1008,1280]{1,0:T(8,128)(2,1)S(1)} %reshape.869, bf16[1280,1280]{1,0:T(8,128)(2,1)} %all-gather.12.cloned.1.call-done, f32[1280]{0:T(1024)S(1)} %copy-done.7), kind=kOutput, calls=%fused_computation.32 | convolution fusion | flops 6620221440 | bytes 11719680 | tf_op jit(solution)/shard_map/imf,fd->imd/dot_general | solution.py:122
  341.7 27.8 %fusion.1 = bf16[256,1280]{1,0:T(8,128)(2,1)S(1)} fusion(bf16[1,1008,1280]{2,1,0:T(8,128)(2,1)} %fusion.20), kind=kCustom, calls=%all-reduce-scatter.1 | all-reduce-scatter fusion | flops 1310721 | bytes 3236352
  369.6 4.4 %collective-permute-start.1 = (bf16[12,1280]{1,0:T(8,128)(2,1)S(1)}, bf16[12,1280]{1,0:T(8,128)(2,1)S(1)}, u32[]{:S(2)}, u32[]{:S(2)}) collective-permute-start(bf16[12,1280]{1,0:T(8,128)(2,1)S(1)} %slice.37), channel_id=1, source_target_pairs={{0,1},{1,2},{2,3},{4,5},{5,6},{6,7},{8,9},{9,10},{10,11},{12,13},{... | collective-permute-start | bytes 92168
  374.0 1.1 collective-permute-done.1
  375.1 1.0 concatenate.5
  376.1 1.3 add_convert_fusion.1
  (22 shorter events, 0.1 us)
Async XLA Ops:
  6.5 5.8 %copy-start = (f32[1,1024]{1,0:T(1,128)S(1)}, f32[1,1024]{1,0:T(1,128)}, u32[]{:S(2)}) copy-start(f32[1,1024]{1,0:T(1,128)} %param.13) | copy-start | bytes 12292
  6.5 5.9 %copy-start.8 = (s32[1,16]{1,0:T(1,128)S(1)}, s32[1,16]{1,0:T(1,128)}, u32[]{:S(2)}) copy-start(s32[1,16]{1,0:T(1,128)} %param.21) | copy-start | bytes 196
  6.5 6.5 %copy-start.3 = (s32[1,1008]{1,0:T(1,128)S(1)}, s32[1,1008]{1,0:T(1,128)}, u32[]{:S(2)}) copy-start(s32[1,1008]{1,0:T(1,128)} %param.23) | copy-start | bytes 12100
  6.5 8.1 %copy-start.5 = (s32[1,16]{1,0:T(1,128)S(1)}, s32[1,16]{1,0:T(1,128)}, u32[]{:S(2)}) copy-start(s32[1,16]{1,0:T(1,128)} %param.22) | copy-start | bytes 196
  6.5 8.3 %copy-start.2 = (bf16[320,160]{0,1:T(8,128)(2,1)S(1)}, bf16[320,160]{0,1:T(8,128)(2,1)}, u32[]{:S(2)}) copy-start(bf16[320,160]{0,1:T(8,128)(2,1)} %param.16) | copy-start | bytes 307204
  6.5 36.6 %all-gather.6.cloned.1.call-start = ((), (), s32[]{:S(2)}) async-start(), calls=%async_computation | async-start | bytes 3276800 | tf_op jit(solution)/shard_map/all_gather | solution.py:48
  11.6 86.2 %all-gather.8.cloned.1.call-start = ((), (), s32[]{:S(2)}) async-start(), calls=%async_computation.1 | async-start | bytes 3317760 | tf_op jit(solution)/shard_map/all_gather | solution.py:54
  12.3 194.2 %all-gather.10.cloned.1.call-start = ((), (), s32[]{:S(2)}) async-start(), calls=%async_computation.2 | async-start | bytes 3276800 | tf_op jit(solution)/shard_map/all_gather | solution.py:113
  113.2 5.8 %copy-start.9 = (f32[4,512,1024]{2,1,0:T(8,128)S(1)}, f32[4,512,1024]{2,1,0:T(8,128)}, u32[]{:S(2)}) copy-start(f32[4,512,1024]{2,1,0:T(8,128)} %get-tuple-element.11) | copy-start | bytes 25165828
  120.7 5.4 %copy-start.1 = (bf16[1,256,1280]{2,1,0:T(8,128)(2,1)S(1)}, bf16[1,256,1280]{2,1,0:T(8,128)(2,1)}, u32[]{:S(2)}) copy-start(bf16[1,256,1280]{2,1,0:T(8,128)(2,1)} %param.12) | copy-start | bytes 1966084
  145.1 31.8 %copy-start.6 = (u32[32]{0:T(128)S(1)}, u32[32]{0:T(128)}, u32[]{:S(2)}) copy-start(u32[32]{0:T(128)} %constant.99) | copy-start | bytes 388
  145.1 35.0 %copy-start.4 = (f32[1280]{0:T(1024)S(1)}, f32[1280]{0:T(1024)}, u32[]{:S(2)}) copy-start(f32[1280]{0:T(1024)} %param.17) | copy-start | bytes 15364
  172.5 5.7 %collective-permute-start = (bf16[12,1280]{1,0:T(8,128)(2,1)S(1)}, bf16[12,1280]{1,0:T(8,128)(2,1)S(1)}, u32[]{:S(2)}, u32[]{:S(2)}) collective-permute-start(bf16[12,1280]{1,0:T(8,128)(2,1)S(1)} %slice.36), channel_id=1, source_target_pairs={{0,1},{1,2},{2,3},{4,5},{5,6},{6,7},{8,9},{9,10},{10,11},{12,13},{... | collective-permute-start | bytes 92168
  181.4 148.7 %copy-start.7 = (f32[1280]{0:T(1024)S(1)}, f32[1280]{0:T(1024)}, u32[]{:S(2)}) copy-start(f32[1280]{0:T(1024)} %param.19) | copy-start | bytes 15364
  181.4 86.4 %all-gather.12.cloned.1.call-start = ((), (), s32[]{:S(2)}) async-start(), calls=%async_computation.3 | async-start | bytes 3686400 | tf_op jit(solution)/shard_map/all_gather | solution.py:118
  182.0 148.0 %all-gather.14.cloned.1.call-start = ((), (), s32[]{:S(2)}) async-start(), calls=%async_computation.4 | async-start | bytes 3686400 | tf_op jit(solution)/shard_map/all_gather | solution.py:125
  369.6 5.5 %collective-permute-start.1 = (bf16[12,1280]{1,0:T(8,128)(2,1)S(1)}, bf16[12,1280]{1,0:T(8,128)(2,1)S(1)}, u32[]{:S(2)}, u32[]{:S(2)}) collective-permute-start(bf16[12,1280]{1,0:T(8,128)(2,1)S(1)} %slice.37), channel_id=1, source_target_pairs={{0,1},{1,2},{2,3},{4,5},{5,6},{6,7},{8,9},{9,10},{10,11},{12,13},{... | collective-permute-start | bytes 92168
Sparse Core Ops, SparseCore 0:
  11.7 27.9 all-gather.5
  41.9 55.8 all-gather.7
  181.5 24.8 all-gather.9
  208.5 59.2 all-gather.11
  269.9 60.1 all-gather.13
